TPU v7x, 32 devices: a whole 2x2x4 slice. The times are simulated.
32 devices in a mesh: patch: 4 (over z), seq: 4 (over y, x), req: 2 (over core).
Axes of the slice: x: 2, y: 2, z: 4, core: 2. Of those that a mesh axis runs over, the one named last changes fastest.
Arguments:
- query: bfloat16 [4, 8, 3584], P(None, ('patch', 'req')), may hold values from -20 to 20
- text_cache: bfloat16 [4, 8, 3072, 1024], P(None, ('patch', 'req'), 'seq'), may hold values from -6 to 6
- text_len: int32 [8], P(('patch', 'req')), may hold values from 0 to 3072
- image_rows: bfloat16 [4, 8192, 1024], P(None, ('patch', 'seq', 'req')), may hold values from -6 to 6
- patch_map: int32 [8192], P(('patch', 'seq', 'req')), may hold values from 0 to 7, as said below
- image_places: int32 [8192], P(('patch', 'seq', 'req')), may hold values from 0 to 1023, as said below
Outputs:
- attended: bfloat16 [4, 8, 3584], P(None, ('patch', 'req'), 'seq')
- image_cache: bfloat16 [4, 8, 1024, 1024], P(None, ('patch', 'req'), 'seq')
Inputs may be any that keep to these rules, and one draw needn't show every extreme that they name: `patch_map`: each aligned block of 256 rows (the rows of one prefill device) holds exactly 32 rows of every request. `image_places`: together with patch_map every pair of request and position occurs exactly once. The rows of a device whose seq index is s have positions from s * 256 to (s + 1) * 256 - 1.
All inputs are finite; a program needn't handle non-finite values.
Results may differ from a plain program's by a relative error of at most 0.0026.
Values may be sent and summed in bfloat16 or wider, within the bound.
A program may use at most 64 MiB of HBM per device.

v0:
```python
import math

import jax
import jax.numpy as jnp
from jax import lax
from jax.sharding import PartitionSpec as P

HEADS = 28
KV_HEADS = 4
HEAD_DIM = 128


def body(query, text_cache, text_len, image_rows, patch_map, image_places):
    layers, req_dev, query_width = query.shape
    text_dev = text_cache.shape[2]
    full_width = text_cache.shape[3]
    kv_width = full_width // 2
    head_dim = HEAD_DIM
    kv_heads = KV_HEADS
    heads = HEADS
    group = heads // kv_heads
    src_rows = image_rows.shape[1]
    patch_count = lax.axis_size("patch")
    req_count = lax.axis_size("req")
    seq_count = lax.axis_size("seq")
    seq_index = lax.axis_index("seq")
    per_source = src_rows // (patch_count * req_count * req_dev)
    band_size = per_source * patch_count * req_count
    scale = 1.0 / math.sqrt(head_dim)
    order = jnp.argsort(patch_map, stable=True)
    grouped = jnp.take(image_rows, order, axis=1)
    grouped_places = jnp.take(image_places, order)
    sending = grouped.reshape(layers, patch_count * req_count, req_dev, per_source, full_width)
    arrived = lax.all_to_all(sending, ("patch", "req"), split_axis=1, concat_axis=3, tiled=True)
    place_send = grouped_places.reshape(patch_count * req_count, req_dev, per_source)
    arrived_places = lax.all_to_all(
        place_send, ("patch", "req"), split_axis=0, concat_axis=2, tiled=True
    )
    image_block = arrived.reshape(layers, req_dev, band_size, full_width)
    local_places = arrived_places.reshape(req_dev, band_size) - seq_index * band_size
    inverse = jnp.argsort(local_places, axis=1)
    image_cache = jnp.take_along_axis(image_block, inverse[None, :, :, None], axis=2)
    queries = query.reshape(layers, req_dev, kv_heads, group, head_dim)
    text_keys = text_cache[..., :kv_width].reshape(layers, req_dev, text_dev, kv_heads, head_dim)
    text_values = text_cache[..., kv_width:].reshape(layers, req_dev, text_dev, kv_heads, head_dim)
    image_keys = image_block[..., :kv_width].reshape(layers, req_dev, band_size, kv_heads, head_dim)
    image_values = image_block[..., kv_width:].reshape(
        layers, req_dev, band_size, kv_heads, head_dim
    )
    positions = seq_index * text_dev + jnp.arange(text_dev, dtype=jnp.int32)
    used = positions[None, :] < text_len[:, None]
    text_raw = (
        jnp.einsum("lrkgd,lrtkd->lrkgt", queries, text_keys, preferred_element_type=jnp.float32)
        * scale
    )
    text_scores = jnp.where(used[None, :, None, None, :], text_raw, -jnp.inf)
    image_scores = (
        jnp.einsum("lrkgd,lrtkd->lrkgt", queries, image_keys, preferred_element_type=jnp.float32)
        * scale
    )
    local_top = jnp.maximum(jnp.max(text_scores, axis=-1), jnp.max(image_scores, axis=-1))
    text_weights = jnp.exp(text_scores - local_top[..., None])
    image_weights = jnp.exp(image_scores - local_top[..., None])
    local_total = jnp.sum(text_weights, axis=-1) + jnp.sum(image_weights, axis=-1)
    text_rounded = text_weights.astype(jnp.bfloat16)
    image_rounded = image_weights.astype(jnp.bfloat16)
    local_values = jnp.einsum(
        "lrkgt,lrtkd->lrkgd", image_rounded, image_values, preferred_element_type=jnp.float32
    )
    local_values = local_values + jnp.einsum(
        "lrkgt,lrtkd->lrkgd", text_rounded, text_values, preferred_element_type=jnp.float32
    )
    width_dev = query_width // seq_count
    top = lax.pmax(local_top, "seq")
    factor = jnp.exp(local_top - top)
    scaled_total = factor * local_total
    scaled_values = factor[..., None] * local_values
    total_sum, value_sum = lax.psum((scaled_total, scaled_values), "seq")
    result = (value_sum / total_sum[..., None]).reshape(layers, req_dev, query_width)
    attended = lax.dynamic_slice_in_dim(result, seq_index * width_dev, width_dev, 2).astype(
        jnp.bfloat16
    )
    return (attended, image_cache)


def solution(mesh):
    return jax.shard_map(
        body,
        mesh=mesh,
        in_specs=(
            P(None, ("patch", "req"), None),
            P(None, ("patch", "req"), "seq", None),
            P(("patch", "req")),
            P(None, ("patch", "seq", "req"), None),
            P(("patch", "seq", "req")),
            P(("patch", "seq", "req")),
        ),
        out_specs=(P(None, ("patch", "req"), "seq"), P(None, ("patch", "req"), "seq", None)),
        check_vma=False,
    )
```

profile of v0, /device:TPU:0, one launch (start us, length us, event | category | flops | bytes accessed | tf_op | source)
XLA Modules:
  0.0 146.9 jit_solution(15871256355636181581)
XLA Ops:
  7.2 0.0 copy-start
  7.2 4.0 %sort.34 = (s32[256]{0:T(256)}, s32[256]{0:T(256)S(1)}) sort(s32[256]{0:T(256)} %param.10, s32[256]{0:T(256)S(1)} %iota.17), dimensions={0}, to_apply=%region_1.2 | sort | flops 2048 | bytes 4096 | tf_op jit(solution)/shard_map/jit(argsort)/sort | solution.py:30
  11.2 2.0 %gather_fusion.1 = s32[256]{0:T(256)S(1)} fusion(s32[256]{0:T(256)} %param.11, s32[1024]{0:T(1024)S(1)} %pad_clamp_fusion.1), kind=kCustom, calls=%fused_computation.1 | custom fusion | bytes 3072 | tf_op jit(solution)/shard_map/jit(_take)/gather | solution.py:32
  13.2 0.7 select_n.78
  13.9 6.4 %all-to-all-start.1 = ((s32[8,1,32]{2,1,0:T(1,128)}), s32[8,1,32]{2,1,0:T(1,128)S(1)}, u32[]{:S(2)}, u32[]{:S(2)}) async-start(s32[8,1,32]{2,1,0:T(1,128)} %select_n.78), calls=%async_computation.1 | async-start | bytes 8192 | tf_op jit(solution)/shard_map/all_to_all | solution.py:36
  20.2 0.0 copy-done
  20.2 8.2 %gather_fusion = bf16[256,4,1024]{2,0,1:T(8,128)(2,1)} fusion(bf16[4,256,1024]{2,1,0:T(8,128)(2,1)S(1)} %copy-done, s32[1024]{0:T(1024)S(1)} %pad_clamp_fusion.1), kind=kCustom, calls=%fused_computation | custom fusion | bytes 4195328 | tf_op jit(solution)/shard_map/jit(_take)/gather | solution.py:31
  28.4 0.1 broadcast_in_dim.54
  28.5 3.3 %copy_select_fusion = bf16[4,8,1,32,1024]{4,3,0,2,1:T(8,128)(2,1)} fusion(bf16[4,8,1,32,1024]{4,3,1,0,2:T(8,128)(2,1)} %bitcast.46, pred[8,32]{1,0:T(8,128)(4,1)S(1)} %broadcast_in_dim.54), kind=kLoop, calls=%fused_computation.4 | loop fusion | flops 1048576 | bytes 4194560 | tf_op jit(solution)/shard_map/jit(_take)/select_n | solution.py:31
  31.7 0.0 copy-start.2
  31.7 0.0 all-to-all-done.1
  31.7 5.2 %all-to-all-start = ((bf16[4,8,1,32,1024]{4,3,0,2,1:T(8,128)(2,1)}), bf16[4,8,1,32,1024]{4,3,0,2,1:T(8,128)(2,1)}, u32[]{:S(2)}, u32[]{:S(2)}) async-start(bf16[4,8,1,32,1024]{4,3,0,2,1:T(8,128)(2,1)} %copy_select_fusion), calls=%async_computation | async-start | bytes 4194304 | tf_op jit(solution)/shard_map/all_to_all | solution.py:34
  37.0 0.0 sort.37.cloned.1.call-start
  37.0 0.0 copy-done.2
  37.1 0.0 copy-start.1
  37.1 5.9 %fusion.15 = (bf16[4,1,768,512]{3,2,1,0:T(8,128)(2,1)}, bf16[4,1,768,512]{3,2,1,0:T(8,128)(2,1)}) fusion(bf16[4,1,768,1024]{3,2,1,0:T(8,128)(2,1)} %param.7), kind=kLoop, calls=%fused_computation.37 | loop fusion | bytes 12582912 | tf_op jit(solution)/shard_map/slice | solution.py:45
  43.0 4.6 %copy.43 = bf16[4,1,768,512]{2,3,0,1:T(8,128)(2,1)} copy(bf16[4,1,768,512]{3,2,1,0:T(8,128)(2,1)} %get-tuple-element.17) | data formatting | bytes 6291456
  48.4 0.6 sub.45
  49.0 0.6 iota.18
  49.6 0.0 sort.37.cloned.1.call-update
  49.6 0.0 copy-done.1
  49.6 2.5 %fusion.17 = (f32[4,4,7]{2,1,0:T(4,128)S(1)}, f32[4,4,7,768]{3,2,1,0:T(8,128)S(1)}) fusion(bf16[4,4,7,128]{3,2,1,0:T(8,128)(2,1)S(1)} %reshape.252, bf16[4,768,4,128]{1,3,2,0:T(8,128)(2,1)} %bitcast.45, pred[768]{0:T(1024)(128)(4,1)S(1)} %add_compare_fusion), kind=kOutput, calls=%fused_computation.39 | convolution fusion | flops 22278032 | bytes 3519680 | tf_op jit(solution)/shard_map/lrkgd,lrtkd->lrkgt/dot_general | solution.py:53
  52.1 4.6 %copy.44 = bf16[4,1,768,512]{2,3,0,1:T(8,128)(2,1)} copy(bf16[4,1,768,512]{3,2,1,0:T(8,128)(2,1)} %get-tuple-element.16) | data formatting | bytes 6291456
  56.7 0.0 sort.37.cloned.1.call-done
  56.7 0.6 compare_select_fusion
  57.3 0.6 pad_clamp_fusion
  57.9 1.1 compare_and_fusion
  59.1 27.0 %all-to-all-done = bf16[4,8,1,32,1024]{4,3,0,2,1:T(8,128)(2,1)} async-done(((bf16[4,8,1,32,1024]{4,3,0,2,1:T(8,128)(2,1)}), bf16[4,8,1,32,1024]{4,3,0,2,1:T(8,128)(2,1)}, u32[]{:S(2)}, u32[]{:S(2)}) %all-to-all-start) | async-done | bytes 2097184 | tf_op jit(solution)/shard_map/all_to_all | solution.py:34
  86.1 1.8 %copy.30 = bf16[4,8,1,32,1024]{4,3,1,0,2:T(8,128)(2,1)S(1)} copy(bf16[4,8,1,32,1024]{4,3,0,2,1:T(8,128)(2,1)} %all-to-all-done) | data formatting | bytes 4194304 | tf_op jit(solution)/shard_map/all_to_all | solution.py:34
  87.9 1.5 %fusion.16 = (bf16[4,1,256,512]{3,2,0,1:T(8,128)(2,1)}, bf16[4,1,256,512]{3,2,0,1:T(8,128)(2,1)}) fusion(bf16[4,1,256,1024]{3,2,0,1:T(8,128)(2,1)S(1)} %bitcast.48), kind=kLoop, calls=%fused_computation.38 | loop fusion | bytes 4194304 | tf_op jit(solution)/shard_map/slice | solution.py:46
  89.4 1.5 %copy.33 = bf16[4,1,256,512]{2,3,0,1:T(8,128)(2,1)S(1)} copy(bf16[4,1,256,512]{3,2,0,1:T(8,128)(2,1)} %get-tuple-element.19) | data formatting | bytes 2097152 | tf_op jit(solution)/shard_map/slice | solution.py:47
  90.9 2.3 %copy.31 = bf16[4,1,256,512]{2,3,0,1:T(8,128)(2,1)} copy(bf16[4,1,256,512]{3,2,0,1:T(8,128)(2,1)} %get-tuple-element.18) | data formatting | bytes 2097152 | tf_op jit(solution)/shard_map/slice | solution.py:46
  93.2 1.6 %fusion.18 = (f32[4,4,7]{2,1,0:T(4,128)S(1)}, f32[4,4,7,256]{3,2,1,0:T(8,128)S(1)}) fusion(bf16[4,256,4,128]{1,3,2,0:T(8,128)(2,1)} %bitcast.50, bf16[4,4,7,128]{3,2,1,0:T(8,128)(2,1)} %copy-done.1), kind=kOutput, calls=%fused_computation.40 | convolution fusion | flops 7397264 | bytes 1192384 | tf_op jit(solution)/shard_map/lrkgd,lrtkd->lrkgt/dot_general | solution.py:58
  94.7 0.2 fusion.8
  94.9 1.1 fusion.10
  96.0 0.2 fusion.4
  96.2 10.3 %pmax.7 = f32[4,1,4,7]{3,2,0,1:T(4,128)S(1)} all-reduce(f32[4,1,4,7]{3,2,0,1:T(4,128)S(1)} %bitcast.51), channel_id=1, replica_groups=mesh['patch'=4,'seq'=4,'req'=2] {'seq'}, use_global_device_ids=true, to_apply=%region_3.4 | all-reduce | flops 112 | bytes 896 | tf_op jit(solution)/shard_map/pmax | solution.py:74
  106.5 2.8 %fusion.3 = f32[4,1,4,7,128]{4,3,2,0,1:T(8,128)S(1)} fusion(f32[4,4,7,128]{3,2,1,0:T(8,128)} %fusion.10, bf16[4,768,4,128]{1,3,2,0:T(8,128)(2,1)} %bitcast.44, f32[4,4,7,768]{3,2,1,0:T(8,128)S(1)} %get-tuple-element.23, f32[4,4,7]{2,1,0:T(4,128)S(1)} %max.20, f32[4,4,7]{2,1,0:T(4,128)S(1)} %get-tuple-element.21), kind=kOutput, calls=%fused_computation.11 | convolution fusion | flops 22220800 | bytes 3605376 | tf_op jit(solution)/shard_map/lrkgt,lrtkd->lrkgd/dot_general | solution.py:70
  109.3 15.4 %all-reduce = (f32[4,1,4,7,128]{4,3,2,0,1:T(8,128)S(1)}, f32[4,4,7]{2,1,0:T(4,128)S(1)}) all-reduce(f32[4,1,4,7,128]{4,3,2,0,1:T(8,128)S(1)} %fusion.3, f32[4,4,7]{2,1,0:T(4,128)S(1)} %get-tuple-element.20), channel_id=1, replica_groups=mesh['patch'=4,'seq'=4,'req'=2] {'seq'}, use_global_device_ids=true, to_apply=%region_4.5 | all-reduce | flops 14448 | bytes 115584 | tf_op jit(solution)/shard_map/psum | solution.py:78
  124.8 0.1 broadcast_divide_fusion
  124.9 4.5 %copy.37 = bf16[4,8,1,32,1024]{4,0,3,1,2:T(4,128)(2,1)} copy(bf16[4,8,1,32,1024]{4,3,0,2,1:T(8,128)(2,1)} %all-to-all-done) | data formatting | bytes 4194304 | tf_op jit(solution)/shard_map/all_to_all | solution.py:34
  129.4 0.0 copy-start.3
  129.4 5.4 %gather_fusion.2 = bf16[256,4,1024]{2,1,0:T(4,128)(2,1)} fusion(bf16[4,256,1024]{2,0,1:T(4,128)(2,1)} %bitcast.47, s32[1024]{0:T(1024)} %pad_clamp_fusion), kind=kCustom, calls=%fused_computation.2 | custom fusion | bytes 4195328 | tf_op jit(solution)/shard_map/jit(take_along_axis)/gather | solution.py:42
  134.9 0.0 copy-done.3
  134.9 2.7 %bitcast_select_fusion = bf16[4,1,256,1024]{3,0,2,1:T(4,128)(2,1)S(1)} fusion(bf16[256,4,1024]{2,1,0:T(4,128)(2,1)} %gather_fusion.2, pred[256]{0:T(512)(128)(4,1)S(1)} %copy-done.3), kind=kLoop, calls=%fused_computation.3 | loop fusion | flops 1048576 | bytes 4194560 | tf_op jit(solution)/shard_map/jit(take_along_axis)/select_n | solution.py:42
  137.5 1.9 %copy.38 = bf16[4,1,256,1024]{3,2,1,0:T(8,128)(2,1)} copy(bf16[4,1,256,1024]{3,0,2,1:T(4,128)(2,1)S(1)} %bitcast_select_fusion) | data formatting | bytes 4194304
  139.5 0.6 dynamic-slice_convert_fusion
  (10 shorter events, 0.1 us)
Async XLA Ops:
  7.2 13.1 %copy-start = (bf16[4,256,1024]{2,1,0:T(8,128)(2,1)S(1)}, bf16[4,256,1024]{2,1,0:T(8,128)(2,1)}, u32[]{:S(2)}) copy-start(bf16[4,256,1024]{2,1,0:T(8,128)(2,1)} %param.9) | copy-start | bytes 6291460
  13.9 17.9 %all-to-all-start.1 = ((s32[8,1,32]{2,1,0:T(1,128)}), s32[8,1,32]{2,1,0:T(1,128)S(1)}, u32[]{:S(2)}, u32[]{:S(2)}) async-start(s32[8,1,32]{2,1,0:T(1,128)} %select_n.78), calls=%async_computation.1 | async-start | bytes 8192 | tf_op jit(solution)/shard_map/all_to_all | solution.py:36
  31.7 5.3 %copy-start.2 = (bf16[4,1,3584]{2,0,1:T(4,128)(2,1)S(1)}, bf16[4,1,3584]{2,0,1:T(4,128)(2,1)}, u32[]{:S(2)}) copy-start(bf16[4,1,3584]{2,0,1:T(4,128)(2,1)} %param.6) | copy-start | bytes 86020
  31.7 54.4 %all-to-all-start = ((bf16[4,8,1,32,1024]{4,3,0,2,1:T(8,128)(2,1)}), bf16[4,8,1,32,1024]{4,3,0,2,1:T(8,128)(2,1)}, u32[]{:S(2)}, u32[]{:S(2)}) async-start(bf16[4,8,1,32,1024]{4,3,0,2,1:T(8,128)(2,1)} %copy_select_fusion), calls=%async_computation | async-start | bytes 4194304 | tf_op jit(solution)/shard_map/all_to_all | solution.py:34
  37.0 19.8 %sort.37.cloned.1.call-start = ((), (), s32[]{:S(2)}) async-start(), calls=%async_computation.2 | async-start | bytes 6176 | tf_op jit(solution)/shard_map/jit(argsort)/sort | solution.py:41
  37.1 12.5 %copy-start.1 = (bf16[4,4,7,128]{3,2,1,0:T(8,128)(2,1)}, bf16[4,4,7,128]{3,2,1,0:T(8,128)(2,1)S(1)}, u32[]{:S(2)}) copy-start(bf16[4,4,7,128]{3,2,1,0:T(8,128)(2,1)S(1)} %reshape.252) | copy-start | bytes 86020
  129.4 5.4 %copy-start.3 = (pred[256]{0:T(512)(128)(4,1)S(1)}, pred[256]{0:T(512)(128)(4,1)}, u32[]{:S(2)}) copy-start(pred[256]{0:T(512)(128)(4,1)} %compare_and_fusion) | copy-start | bytes 772
Sparse Core Ops, SparseCore 0:
  49.7 2.5 sort.39.cloned.1.call-done
  (1 shorter events, 0.0 us)
where the time goes:
time: 148 us; the launch traced here: 147 us
  local copies, waits for them, and re-layouts  47 us (32%)
  waiting for transfers between devices  27 us (18%)
  blocking collectives  25.7 us (17%)
  between operations  14.8 us (10%)
  other arithmetic  12.8 us (9%)
  starting transfers between devices  11.6 us (8%)
  matrix products  7.95 us (5%)
    all_to_all x1, waiting for transfers between devices, body(): lax.all_to_all(sending, ('patch', 'req'), split_axis=1, concat_axis=3, ti...  27 us
    psum x1, blocking collectives, body(): total_sum, value_sum = lax.psum((scaled_total, scaled_values), 'seq')  15.4 us
    unnamed x12, local copies, waits for them, and re-layouts  11.3 us
    pmax x1, blocking collectives, body(): top = lax.pmax(local_top, 'seq')  10.3 us
    gather x1, local copies, waits for them, and re-layouts, body(): grouped = jnp.take(image_rows, order, axis=1)  8.15 us
    all_to_all x1, starting transfers between devices, body(): lax.all_to_all(place_send, ('patch', 'req'), split_axis=0, concat_axis=2,...  6.35 us
    all_to_all x2, local copies, waits for them, and re-layouts, body(): lax.all_to_all(sending, ('patch', 'req'), split_axis=1, concat_axis=3, ti...  6.3 us
    slice x1, local copies, waits for them, and re-layouts, body(): text_cache[..., kv_width:]  5.94 us
  transfers between devices with their start and end apart: 2, of which 1 were waited for; matrix products, arithmetic and copies ran while one was open for 22% of the time, Pallas kernels for 0%

commit v1 on v0

v1 whole, which is shorter than its diff:
```python
import functools
import math

import jax
import jax.numpy as jnp
from jax import lax
from jax.experimental import pallas as pl
from jax.experimental.pallas import tpu as pltpu
from jax.sharding import PartitionSpec as P

HEADS = 28
KV_HEADS = 4
HEAD_DIM = 128
PAD = 8
MESH = pl.DeviceIdType.MESH
NT = (((1,), (1,)), ((), ()))


def hop_order(patch_count, req_count):
    steps = sorted(range(1, patch_count), key=lambda d: -min(d, patch_count - d))
    pairs = [(d, c) for d in steps for c in range(req_count)]
    return pairs + [(0, c) for c in range(1, req_count)]


def kernel(
    dims,
    query_ref, len_ref, map_ref, place_ref, rows_hbm, text_hbm,
    att_ref, cache_hbm,
    rows, text, grouped, arrived, cache, place_out, place_in, scores, part_out, part_in,
    rows_sem, text_sem, cache_sem, img_send, img_recv, place_send, place_recv,
    part_send, part_recv,
):
    patch_count, seq_count, req_count = dims
    layers, src_rows, full = rows.shape
    text_dev = text.shape[1]
    kvw = full // 2
    group = HEADS // KV_HEADS
    groups = patch_count * req_count
    per = src_rows // groups
    scale = 1.0 / math.sqrt(HEAD_DIM)
    patch, seq, req = (lax.axis_index(a) for a in ("patch", "seq", "req"))
    me = patch * req_count + req
    hops = hop_order(patch_count, req_count)

    for l in range(layers):
        pltpu.make_async_copy(rows_hbm.at[l], rows.at[l], rows_sem.at[l]).start()
    for l in range(layers):
        pltpu.make_async_copy(text_hbm.at[l, 0], text.at[l], text_sem.at[l]).start()

    def partner(hop):
        p = lax.rem(patch + hop[0], patch_count)
        r = lax.rem(req + hop[1], req_count)
        return p, r

    barrier = pltpu.get_barrier_semaphore()
    for hop in hops:
        p, r = partner(hop)
        pl.semaphore_signal(barrier, inc=1, device_id=(p, seq, r), device_id_type=MESH)
    for d in range(1, seq_count):
        s = lax.rem(seq + d, seq_count)
        pl.semaphore_signal(barrier, inc=1, device_id=(patch, s, req), device_id_type=MESH)

    f32, bf16 = jnp.float32, jnp.bfloat16
    owner = lax.broadcasted_iota(jnp.int32, (groups, src_rows), 0)
    mine = map_ref[...] == owner
    row_i = lax.broadcasted_iota(jnp.int32, (src_rows, src_rows), 0)
    col_i = lax.broadcasted_iota(jnp.int32, (src_rows, src_rows), 1)
    before = (row_i < col_i).astype(f32).astype(bf16)
    rank = jnp.dot(mine.astype(f32).astype(bf16), before, preferred_element_type=f32)
    slot = jnp.sum(
        jnp.where(mine, rank + (owner * per).astype(f32), 0.0), axis=0, keepdims=True
    )
    pick = (row_i == slot.astype(jnp.int32)).astype(f32).astype(bf16)
    local = (place_ref[...] - seq * src_rows).astype(f32).astype(bf16)
    place_sorted = lax.dot_general(
        jnp.broadcast_to(local, (PAD, src_rows)), pick, NT, preferred_element_type=f32
    )
    place_out[...] = place_sorted[0:1].astype(jnp.int32)
    place_in[me] = place_sorted[0:1].astype(jnp.int32)

    pl.semaphore_wait(barrier, len(hops) + seq_count - 1)

    def place_copy(k, hop):
        p, r = partner(hop)
        return pltpu.make_async_remote_copy(
            src_ref=place_out, dst_ref=place_in.at[me],
            send_sem=place_send.at[k], recv_sem=place_recv.at[k],
            device_id=(p, seq, r), device_id_type=MESH,
        )

    def image_copy(l, k, hop):
        p, r = partner(hop)
        return pltpu.make_async_remote_copy(
            src_ref=grouped.at[l, p * req_count + r], dst_ref=arrived.at[l, me],
            send_sem=img_send.at[l, k], recv_sem=img_recv.at[l, k],
            device_id=(p, seq, r), device_id_type=MESH,
        )

    def part_copy(l, d):
        s = lax.rem(seq + d, seq_count)
        return pltpu.make_async_remote_copy(
            src_ref=part_out.at[l, s], dst_ref=part_in.at[l, d],
            send_sem=part_send.at[l, d], recv_sem=part_recv.at[l, d],
            device_id=(patch, s, req), device_id_type=MESH,
        )

    for l in range(layers):
        pltpu.make_async_copy(rows_hbm.at[l], rows.at[l], rows_sem.at[l]).wait()
        moved = jnp.dot(pick, rows[l], preferred_element_type=f32).astype(bf16)
        grouped[l] = moved.reshape(groups, per, full)
        if l == 0:
            for k, hop in enumerate(hops):
                place_copy(k, hop).start()
        for k, hop in enumerate(hops):
            image_copy(l, k, hop).start()
    for l in range(layers):
        arrived[l, me] = grouped[l, me]

    positions = seq * text_dev + lax.broadcasted_iota(
        jnp.int32, (KV_HEADS * PAD, text_dev), 1
    )
    used = positions < len_ref[0]
    zeros = jnp.zeros((PAD, HEAD_DIM), bf16)
    spread = []
    for l in range(layers):
        line = query_ref[l].astype(f32)
        blocks = []
        for g in range(KV_HEADS):
            heads = [
                line[:, (g * group + h) * HEAD_DIM:(g * group + h + 1) * HEAD_DIM]
                for h in range(group)
            ] + [jnp.zeros((PAD - group, HEAD_DIM), f32)]
            block = jnp.concatenate(heads, axis=0).astype(bf16)
            blocks.append(
                jnp.concatenate(
                    [block if c == g else zeros for c in range(KV_HEADS)], axis=1
                )
            )
        spread.append(jnp.concatenate(blocks, axis=0))
    for l in range(layers):
        pltpu.make_async_copy(text_hbm.at[l, 0], text.at[l], text_sem.at[l]).wait()
        raw = lax.dot_general(
            spread[l], text[l, :, :kvw], NT, preferred_element_type=f32
        ) * scale
        scores[l] = jnp.where(used, raw, -jnp.inf)

    for k, hop in enumerate(hops):
        place_copy(k, hop).wait_recv()
    wanted = (row_i == me * per + lax.rem(col_i, per)).astype(f32).astype(bf16)
    lanes = jnp.dot(
        place_in[...].reshape(groups, src_rows).astype(f32).astype(bf16), wanted,
        preferred_element_type=f32,
    )
    source = lax.broadcasted_iota(jnp.int32, (groups, src_rows), 1) // per
    place = jnp.sum(jnp.where(source == owner, lanes, 0.0), axis=0, keepdims=True)
    put = (row_i == place.astype(jnp.int32)).astype(f32).astype(bf16)

    for l in range(layers):
        for k, hop in enumerate(hops):
            image_copy(l, k, hop).wait_recv()
        block = arrived[l].reshape(src_rows, full)
        image_scores = lax.dot_general(
            spread[l], block[:, :kvw], NT, preferred_element_type=f32
        ) * scale
        text_scores = scores[l]
        top = jnp.maximum(
            jnp.max(text_scores, axis=1, keepdims=True),
            jnp.max(image_scores, axis=1, keepdims=True),
        )
        text_w = jnp.exp(text_scores - top)
        image_w = jnp.exp(image_scores - top)
        total = jnp.sum(text_w, axis=1, keepdims=True) + jnp.sum(
            image_w, axis=1, keepdims=True
        )
        values = jnp.dot(
            image_w.astype(bf16), block[:, kvw:], preferred_element_type=f32
        ) + jnp.dot(text_w.astype(bf16), text[l, :, kvw:], preferred_element_type=f32)
        for g in range(KV_HEADS):
            at = slice(g * PAD, (g + 1) * PAD)
            cell = jnp.concatenate(
                [
                    values[at, g * HEAD_DIM:(g + 1) * HEAD_DIM],
                    jnp.broadcast_to(top[at], (PAD, HEAD_DIM)),
                    jnp.broadcast_to(total[at], (PAD, HEAD_DIM)),
                ],
                axis=1,
            )
            part_out[l, g] = cell
        for d in range(1, seq_count):
            part_copy(l, d).start()
        cache[l] = jnp.dot(put, block, preferred_element_type=f32).astype(bf16)
        pltpu.make_async_copy(cache.at[l], cache_hbm.at[l, 0], cache_sem.at[l]).start()

    for l in range(layers):
        for d in range(1, seq_count):
            part_copy(l, d).wait_recv()
        cells = [part_out[l, seq]] + [part_in[l, d] for d in range(1, seq_count)]
        tops = [c[:, HEAD_DIM:2 * HEAD_DIM] for c in cells]
        top = functools.reduce(jnp.maximum, tops)
        factors = [jnp.exp(t - top) for t in tops]
        total = sum(f * c[:, 2 * HEAD_DIM:] for f, c in zip(factors, cells))
        summed = sum(f * c[:, :HEAD_DIM] for f, c in zip(factors, cells))
        result = summed / total
        att_ref[l] = jnp.concatenate(
            [result[h:h + 1] for h in range(group)], axis=1
        ).astype(bf16)

    for l in range(layers):
        pltpu.make_async_copy(cache.at[l], cache_hbm.at[l, 0], cache_sem.at[l]).wait()
        for k, hop in enumerate(hops):
            image_copy(l, k, hop).wait_send()
        for d in range(1, seq_count):
            part_copy(l, d).wait_send()
    for k, hop in enumerate(hops):
        place_copy(k, hop).wait_send()


def body(dims, query, text_cache, text_len, image_rows, patch_map, image_places):
    patch_count, seq_count, req_count = dims
    layers, req_dev, query_width = query.shape
    text_dev, full = text_cache.shape[2:]
    src_rows = image_rows.shape[1]
    groups = patch_count * req_count
    assert req_dev == 1 and seq_count == KV_HEADS and full == 2 * KV_HEADS * HEAD_DIM
    per = src_rows // groups
    hops = groups - 1
    bf16, f32 = jnp.bfloat16, jnp.float32
    dma = pltpu.SemaphoreType.DMA
    vmem = pl.BlockSpec(memory_space=pltpu.VMEM)
    hbm = pl.BlockSpec(memory_space=pl.ANY)
    return pl.pallas_call(
        functools.partial(kernel, dims),
        out_shape=(
            jax.ShapeDtypeStruct((layers, 1, query_width // seq_count), bf16),
            jax.ShapeDtypeStruct((layers, 1, src_rows, full), bf16),
        ),
        in_specs=[vmem, pl.BlockSpec(memory_space=pltpu.SMEM), vmem, vmem, hbm, hbm],
        out_specs=(vmem, hbm),
        scratch_shapes=[
            pltpu.VMEM((layers, src_rows, full), bf16),
            pltpu.VMEM((layers, text_dev, full), bf16),
            pltpu.VMEM((layers, groups, per, full), bf16),
            pltpu.VMEM((layers, groups, per, full), bf16),
            pltpu.VMEM((layers, src_rows, full), bf16),
            pltpu.VMEM((1, src_rows), jnp.int32),
            pltpu.VMEM((groups, 1, src_rows), jnp.int32),
            pltpu.VMEM((layers, KV_HEADS * PAD, text_dev), f32),
            pltpu.VMEM((layers, KV_HEADS, PAD, 3 * HEAD_DIM), f32),
            pltpu.VMEM((layers, seq_count, PAD, 3 * HEAD_DIM), f32),
            dma((layers,)), dma((layers,)), dma((layers,)),
            dma((layers, hops)), dma((layers, hops)), dma((hops,)), dma((hops,)),
            dma((layers, seq_count)), dma((layers, seq_count)),
        ],
        compiler_params=pltpu.CompilerParams(
            collective_id=0, has_side_effects=True, vmem_limit_bytes=48 * 1024 * 1024
        ),
    )(
        query, text_len, patch_map.reshape(1, src_rows), image_places.reshape(1, src_rows),
        image_rows, text_cache,
    )


def solution(mesh):
    dims = tuple(mesh.shape[a] for a in ("patch", "seq", "req"))
    return jax.shard_map(
        functools.partial(body, dims),
        mesh=mesh,
        in_specs=(
            P(None, ("patch", "req"), None),
            P(None, ("patch", "req"), "seq", None),
            P(("patch", "req")),
            P(None, ("patch", "seq", "req"), None),
            P(("patch", "seq", "req")),
            P(("patch", "seq", "req")),
        ),
        out_specs=(P(None, ("patch", "req"), "seq"), P(None, ("patch", "req"), "seq", None)),
        check_vma=False,
    )
```

time: 148 us -> 62.7 us (0.42)
  Pallas kernels: 0 us -> 55.2 us
  local copies, waits for them, and re-layouts: 47 us -> 5.65 us
  waiting for transfers between devices: 27 us -> 0 us
  blocking collectives: 25.7 us -> 0 us
  between operations: 14.8 us -> 1.3 us
  other arithmetic: 12.8 us -> 0 us
  starting transfers between devices: 11.6 us -> 0 us
  matrix products: 7.95 us -> 0 us
    pallas_call x0 -> x1, Pallas kernels: none -> 55.2 us  [body(): pl.pallas_call(functools.partial(kernel, dims), out_shape=(jax.ShapeDtype...]
    all_to_all x2 -> x0, waiting for transfers between devices: 27 us -> none  [the longest x1 27 us: body(): lax.all_to_all(sending, ('patch', 'req'), split_axis=1, concat_axis=3, ti...]
    gather x3 -> x0, local copies, waits for them, and re-layouts: 15.5 us -> none  [the longest x1 8.15 us: body(): grouped = jnp.take(image_rows, order, axis=1)]
    psum x1 -> x0, blocking collectives: 15.4 us -> none  [body(): total_sum, value_sum = lax.psum((scaled_total, scaled_values), 'seq')]
    all_to_all x2 -> x0, starting transfers between devices: 11.6 us -> none  [the longest x1 6.35 us: body(): lax.all_to_all(place_send, ('patch', 'req'), split_axis=0, concat_axis=2,...]
    slice x4 -> x0, local copies, waits for them, and re-layouts: 11.2 us -> none  [the longest x1 5.94 us: body(): text_cache[..., kv_width:]]
    pmax x1 -> x0, blocking collectives: 10.3 us -> none  [body(): top = lax.pmax(local_top, 'seq')]
    dot_general x4 -> x0, matrix products: 7.95 us -> none  [the longest x1 2.84 us: body(): jnp.einsum('lrkgt,lrtkd->lrkgd', text_rounded, text_values, preferred_ele...]
  transfers between devices with their start and end apart: 2 -> 0, of which waited for: 1 -> 0; matrix products, arithmetic and copies ran while one was open for 22% -> 0% of each run, Pallas kernels for 0% -> 0%
where the time goes in v1:
time: 62.7 us; the launch traced here: 62.2 us
  Pallas kernels  55.2 us (88%)
  local copies, waits for them, and re-layouts  5.65 us (9%)
  between operations  1.3 us (2%)
    pallas_call x1, Pallas kernels, body(): pl.pallas_call(functools.partial(kernel, dims), out_shape=(jax.ShapeDtype...  55.2 us
    unnamed x8, local copies, waits for them, and re-layouts  5.06 us

profile of v1, /device:TPU:0, one launch (start us, length us, event | category | flops | bytes accessed | tf_op | source)
XLA Modules:
  0.0 62.2 jit_solution(1096628336297599944)
XLA Ops:
  1.3 0.8 %copy.8.query_ref = bf16[4,1,3584]{2,1,0:T(2,128)(2,1)S(1)} copy(bf16[4,1,3584]{2,0,1:T(4,128)(2,1)} %param.6) | data formatting | bytes 57344 | tf_op args[0]
  2.1 0.0 copy-start
  2.1 1.6 %copy-done = bf16[4,256,1024]{2,1,0:T(8,128)(2,1)S(1)} copy-done((bf16[4,256,1024]{2,1,0:T(8,128)(2,1)S(1)}, bf16[4,256,1024]{2,1,0:T(8,128)(2,1)}, u32[]{:S(2)}) %copy-start) | copy-done | bytes 2097176
  3.7 0.0 copy-start.1
  3.7 0.7 %copy-done.1 = s32[256]{0:T(256)S(1)} copy-done((s32[256]{0:T(256)S(1)}, s32[256]{0:T(256)}, u32[]{:S(2)}) %copy-start.1) | copy-done | bytes 1048
  4.3 0.0 copy-start.2
  4.3 0.7 %copy-done.2 = s32[256]{0:T(256)S(1)} copy-done((s32[256]{0:T(256)S(1)}, s32[256]{0:T(256)}, u32[]{:S(2)}) %copy-start.2) | copy-done | bytes 1048
  5.0 55.2 %shard_map.77 = (bf16[4,1,896]{2,1,0:T(2,128)(2,1)S(1)}, bf16[4,1,256,1024]{3,2,1,0:T(8,128)(2,1)S(1)}) custom-call(bf16[4,1,3584]{2,1,0:T(2,128)(2,1)S(1)} %copy.8.query_ref, s32[1]{0:T(128)S(6)} %copy.11.len_ref, s32[1,256]{1,0:T(1,128)S(1)} %bitcast.2, s32[1,256]{1,0:T(1,128)S(1)} %bitcast.3, bf16[4,256,1024]{2,1,0:T(8,128)(2,1)S(1)} %copy-done, ...), custom_call_target="tpu_custom_call" | custom-call | tf_op jit(solution)/shard_map/pallas_call | solution.py:231
  60.2 0.6 copy.9
  60.8 1.3 %copy.12 = bf16[4,1,256,1024]{3,2,1,0:T(8,128)(2,1)} copy(bf16[4,1,256,1024]{3,2,1,0:T(8,128)(2,1)S(1)} %get-tuple-element.7) | data formatting | bytes 4194304
Async XLA Ops:
  2.1 1.6 %copy-start = (bf16[4,256,1024]{2,1,0:T(8,128)(2,1)S(1)}, bf16[4,256,1024]{2,1,0:T(8,128)(2,1)}, u32[]{:S(2)}) copy-start(bf16[4,256,1024]{2,1,0:T(8,128)(2,1)} %rows_hbm.1) | copy-start | bytes 6291460
  3.7 0.7 %copy-start.1 = (s32[256]{0:T(256)S(1)}, s32[256]{0:T(256)}, u32[]{:S(2)}) copy-start(s32[256]{0:T(256)} %param.10) | copy-start | bytes 3076
  4.3 0.7 %copy-start.2 = (s32[256]{0:T(256)S(1)}, s32[256]{0:T(256)}, u32[]{:S(2)}) copy-start(s32[256]{0:T(256)} %param.11) | copy-start | bytes 3076

commit v2 on v1

v2 whole, which is shorter than its diff:
```python
import functools
import math

import jax
import jax.numpy as jnp
from jax import lax
from jax.experimental import pallas as pl
from jax.experimental.pallas import tpu as pltpu
from jax.sharding import PartitionSpec as P

HEADS = 28
KV_HEADS = 4
HEAD_DIM = 128
PAD = 8
MESH = pl.DeviceIdType.MESH
NT = (((1,), (1,)), ((), ()))


def hop_order(patch_count, req_count):
    steps = sorted(range(1, patch_count), key=lambda d: -min(d, patch_count - d))
    pairs = [(d, c) for d in steps for c in range(req_count)]
    return pairs + [(0, c) for c in range(1, req_count)]


def kernel(
    dims,
    query_ref, len_ref, map_hbm, place_hbm, rows_hbm, text_hbm,
    att_ref, cache,
    query, maps, places, rows, text, main_out, main_in, own_out, own_in, place_out, place_in,
    scores, image_ws, text_sums, image_sums, part_out, part_in,
    small_sem, rows_sem, text_sem, main_send, main_recv, own_send, own_recv,
    place_send, place_recv, part_send, part_recv,
):
    patch_count, seq_count, req_count = dims
    layers, src_rows, full = rows.shape
    text_dev = text.shape[1]
    kvw = full // 2
    group = HEADS // KV_HEADS
    groups = patch_count * req_count
    per = src_rows // groups
    main_width = full - HEAD_DIM
    scale = 1.0 / math.sqrt(HEAD_DIM)
    patch, seq, req = (lax.axis_index(a) for a in ("patch", "seq", "req"))
    me = patch * req_count + req
    hops = hop_order(patch_count, req_count)
    f32, bf16 = jnp.float32, jnp.bfloat16

    small = [
        pltpu.make_async_copy(map_hbm, maps, small_sem.at[0]),
        pltpu.make_async_copy(place_hbm, places, small_sem.at[1]),
        pltpu.make_async_copy(query_ref, query, small_sem.at[2]),
    ]
    for copy in small:
        copy.start()

    def rows_copy(l):
        return pltpu.make_async_copy(rows_hbm.at[l], rows.at[l], rows_sem.at[l])

    def text_copy(l):
        return pltpu.make_async_copy(text_hbm.at[l, 0], text.at[l], text_sem.at[l])

    for l in range(layers):
        rows_copy(l).start()
    for l in range(layers):
        text_copy(l).start()

    def partner(hop):
        p = lax.rem(patch + hop[0], patch_count)
        r = lax.rem(req + hop[1], req_count)
        return p, r

    def lanes_of(d):
        g = lax.rem(seq + d, seq_count)
        return pl.ds(pl.multiple_of(kvw + g * HEAD_DIM, HEAD_DIM), HEAD_DIM)

    barrier = pltpu.get_barrier_semaphore()
    for hop in hops:
        p, r = partner(hop)
        pl.semaphore_signal(barrier, inc=1, device_id=(p, seq, r), device_id_type=MESH)
    for d in range(1, seq_count):
        s = lax.rem(seq + d, seq_count)
        pl.semaphore_signal(barrier, inc=1, device_id=(patch, s, req), device_id_type=MESH)

    owner = lax.broadcasted_iota(jnp.int32, (groups, src_rows), 0)
    row_i = lax.broadcasted_iota(jnp.int32, (src_rows, src_rows), 0)
    col_i = lax.broadcasted_iota(jnp.int32, (src_rows, src_rows), 1)
    before = (row_i < col_i).astype(f32).astype(bf16)
    small[0].wait()
    mine = maps[...] == owner
    rank = jnp.dot(mine.astype(f32).astype(bf16), before, preferred_element_type=f32)
    slot = jnp.sum(
        jnp.where(mine, rank + (owner * per).astype(f32), 0.0), axis=0, keepdims=True
    )
    pick = (row_i == slot.astype(jnp.int32)).astype(f32).astype(bf16)

    def place_copy(k, hop):
        p, r = partner(hop)
        return pltpu.make_async_remote_copy(
            src_ref=place_out, dst_ref=place_in.at[me],
            send_sem=place_send.at[k], recv_sem=place_recv.at[k],
            device_id=(p, seq, r), device_id_type=MESH,
        )

    def main_copy(l, k, hop):
        p, r = partner(hop)
        return pltpu.make_async_remote_copy(
            src_ref=main_out.at[l, p * req_count + r], dst_ref=main_in.at[l, me],
            send_sem=main_send.at[l, k], recv_sem=main_recv.at[l, k],
            device_id=(p, seq, r), device_id_type=MESH,
        )

    def own_copy(k, hop):
        p, r = partner(hop)
        return pltpu.make_async_remote_copy(
            src_ref=own_out.at[p * req_count + r], dst_ref=own_in.at[me],
            send_sem=own_send.at[k], recv_sem=own_recv.at[k],
            device_id=(p, seq, r), device_id_type=MESH,
        )

    def part_copy(l, d):
        s = lax.rem(seq + d, seq_count)
        return pltpu.make_async_remote_copy(
            src_ref=part_out.at[l, d], dst_ref=part_in.at[l, d],
            send_sem=part_send.at[l, d], recv_sem=part_recv.at[l, d],
            device_id=(patch, s, req), device_id_type=MESH,
        )

    for l in range(layers):
        rows_copy(l).wait()
        keys = jnp.dot(pick, rows[l, :, :kvw], preferred_element_type=f32).astype(bf16)
        main_out[l, :, :, :kvw] = keys.reshape(groups, per, kvw)
        others = jnp.concatenate(
            [rows[l, :, lanes_of(d)] for d in range(1, seq_count)] + [rows[l, :, lanes_of(0)]],
            axis=1,
        )
        moved = jnp.dot(pick, others, preferred_element_type=f32).astype(bf16)
        cut = main_width - kvw
        main_out[l, :, :, kvw:] = moved[:, :cut].reshape(groups, per, cut)
        own_out[:, l] = moved[:, cut:].reshape(groups, per, HEAD_DIM)
        if l == 0:
            pl.semaphore_wait(barrier, len(hops) + seq_count - 1)
        for k, hop in enumerate(hops):
            main_copy(l, k, hop).start()
        if l == 0:
            small[1].wait()
            local = (places[...] - seq * src_rows).astype(f32).astype(bf16)
            place_sorted = lax.dot_general(
                jnp.broadcast_to(local, (PAD, src_rows)), pick, NT,
                preferred_element_type=f32,
            )
            place_out[...] = place_sorted[0:1].astype(jnp.int32)
            place_in[me] = place_sorted[0:1].astype(jnp.int32)
            for k, hop in enumerate(hops):
                place_copy(k, hop).start()
    for k, hop in enumerate(hops):
        own_copy(k, hop).start()
    for l in range(layers):
        main_in[l, me] = main_out[l, me]
    own_in[me] = own_out[me]

    positions = seq * text_dev + lax.broadcasted_iota(
        jnp.int32, (KV_HEADS * PAD, text_dev), 1
    )
    used = positions < len_ref[0]
    zeros = jnp.zeros((PAD, HEAD_DIM), bf16)
    small[2].wait()
    lines = query[...].astype(f32)
    spread = []
    for l in range(layers):
        blocks = []
        for g in range(KV_HEADS):
            heads = [
                lines[l:l + 1, (g * group + h) * HEAD_DIM:(g * group + h + 1) * HEAD_DIM]
                for h in range(group)
            ] + [jnp.zeros((PAD - group, HEAD_DIM), f32)]
            block = jnp.concatenate(heads, axis=0).astype(bf16)
            blocks.append(
                jnp.concatenate(
                    [block if c == g else zeros for c in range(KV_HEADS)], axis=1
                )
            )
        spread.append(jnp.concatenate(blocks, axis=0))
    for l in range(layers):
        text_copy(l).wait()
        raw = lax.dot_general(
            spread[l], text[l, :, :kvw], NT, preferred_element_type=f32
        ) * scale
        scores[l] = jnp.where(used, raw, -jnp.inf)

    for k, hop in enumerate(hops):
        place_copy(k, hop).wait_recv()
    wanted = (row_i == me * per + lax.rem(col_i, per)).astype(f32).astype(bf16)
    lanes = jnp.dot(
        place_in[...].reshape(groups, src_rows).astype(f32).astype(bf16), wanted,
        preferred_element_type=f32,
    )
    source = lax.broadcasted_iota(jnp.int32, (groups, src_rows), 1) // per
    place = jnp.sum(jnp.where(source == owner, lanes, 0.0), axis=0, keepdims=True)
    put = (row_i == place.astype(jnp.int32)).astype(f32).astype(bf16)

    for l in range(layers):
        for k, hop in enumerate(hops):
            main_copy(l, k, hop).wait_recv()
        block = main_in[l].reshape(src_rows, main_width)
        image_scores = lax.dot_general(
            spread[l], block[:, :kvw], NT, preferred_element_type=f32
        ) * scale
        text_scores = scores[l]
        top = jnp.maximum(
            jnp.max(text_scores, axis=1, keepdims=True),
            jnp.max(image_scores, axis=1, keepdims=True),
        )
        text_w = jnp.exp(text_scores - top)
        image_w = jnp.exp(image_scores - top)
        total = jnp.sum(text_w, axis=1, keepdims=True) + jnp.sum(
            image_w, axis=1, keepdims=True
        )
        text_sums[:, :kvw] = jnp.dot(
            text_w.astype(bf16), text[l, :, kvw:], preferred_element_type=f32
        )
        text_sums[:, kvw:kvw + HEAD_DIM] = jnp.broadcast_to(top, (KV_HEADS * PAD, HEAD_DIM))
        text_sums[:, kvw + HEAD_DIM:] = jnp.broadcast_to(total, (KV_HEADS * PAD, HEAD_DIM))
        image_sums[...] = jnp.dot(
            image_w.astype(bf16), block[:, kvw:], preferred_element_type=f32
        )
        image_ws[l] = image_w
        for d in range(seq_count):
            g = lax.rem(seq + d, seq_count)
            at = pl.ds(pl.multiple_of(g * PAD, PAD), PAD)
            value = text_sums[at, pl.ds(pl.multiple_of(g * HEAD_DIM, HEAD_DIM), HEAD_DIM)]
            if d:
                value = value + image_sums[at, (d - 1) * HEAD_DIM:d * HEAD_DIM]
            part_out[l, d, :, :HEAD_DIM] = value
            part_out[l, d, :, HEAD_DIM:] = text_sums[at, kvw:]
            if d:
                part_copy(l, d).start()
        moved = jnp.dot(put, block, preferred_element_type=f32).astype(bf16)
        cache[l, 0, :, :kvw] = moved[:, :kvw]
        for d in range(1, seq_count):
            cache[l, 0, :, lanes_of(d)] = moved[
                :, kvw + (d - 1) * HEAD_DIM:kvw + d * HEAD_DIM
            ]

    partial = []
    for l in range(layers):
        for d in range(1, seq_count):
            part_copy(l, d).wait_recv()
        cells = [part_out[l, 0]] + [part_in[l, d] for d in range(1, seq_count)]
        tops = [c[:, HEAD_DIM:2 * HEAD_DIM] for c in cells]
        top = functools.reduce(jnp.maximum, tops)
        factors = [jnp.exp(t - top) for t in tops]
        total = sum(f * c[:, 2 * HEAD_DIM:] for f, c in zip(factors, cells))
        summed = sum(f * c[:, :HEAD_DIM] for f, c in zip(factors, cells))
        partial.append((factors[0], summed, total))

    for k, hop in enumerate(hops):
        own_copy(k, hop).wait_recv()
    at = pl.ds(pl.multiple_of(seq * PAD, PAD), PAD)
    own_values = [own_in[:, l].reshape(src_rows, HEAD_DIM) for l in range(layers)]
    lines = []
    for l in range(layers):
        factor, summed, total = partial[l]
        value = jnp.dot(
            image_ws[l, at, :].astype(bf16), own_values[l], preferred_element_type=f32
        )
        result = (summed + factor * value) / total
        lines.append(jnp.concatenate([result[h:h + 1] for h in range(group)], axis=1))
    att_ref[...] = jnp.concatenate(lines, axis=0).astype(bf16)
    moved = jnp.dot(
        put, jnp.concatenate(own_values, axis=1), preferred_element_type=f32
    ).astype(bf16)
    for l in range(layers):
        cache[l, 0, :, lanes_of(0)] = moved[:, l * HEAD_DIM:(l + 1) * HEAD_DIM]

    for l in range(layers):
        for k, hop in enumerate(hops):
            main_copy(l, k, hop).wait_send()
        for d in range(1, seq_count):
            part_copy(l, d).wait_send()
    for k, hop in enumerate(hops):
        own_copy(k, hop).wait_send()
        place_copy(k, hop).wait_send()


def finish(att_ref, cache_ref, att_out, cache_out, sem):
    layers = cache_ref.shape[0]
    copies = [
        pltpu.make_async_copy(cache_ref.at[l], cache_out.at[l], sem.at[l])
        for l in range(layers)
    ]
    for copy in copies:
        copy.start()
    att_out[...] = att_ref[...]
    for copy in copies:
        copy.wait()


def body(dims, query, text_cache, text_len, image_rows, patch_map, image_places):
    patch_count, seq_count, req_count = dims
    layers, req_dev, query_width = query.shape
    text_dev, full = text_cache.shape[2:]
    src_rows = image_rows.shape[1]
    groups = patch_count * req_count
    assert req_dev == 1 and seq_count == KV_HEADS and full == 2 * KV_HEADS * HEAD_DIM
    per = src_rows // groups
    hops = groups - 1
    kvw = full // 2
    main_width = full - HEAD_DIM
    rows_padded = KV_HEADS * PAD
    bf16, f32, i32 = jnp.bfloat16, jnp.float32, jnp.int32
    dma = pltpu.SemaphoreType.DMA
    vmem = pl.BlockSpec(memory_space=pltpu.VMEM)
    hbm = pl.BlockSpec(memory_space=pltpu.HBM)
    att_shape = jax.ShapeDtypeStruct((layers, query_width // seq_count), bf16)
    cache_shape = jax.ShapeDtypeStruct((layers, 1, src_rows, full), bf16)
    in_hbm = lambda x: pltpu.with_memory_space_constraint(x, pltpu.HBM)
    in_vmem = lambda x: pltpu.with_memory_space_constraint(x, pltpu.VMEM)
    attended, cache = pl.pallas_call(
        functools.partial(kernel, dims),
        out_shape=(
            pltpu.VMEM(att_shape.shape, bf16), pltpu.VMEM(cache_shape.shape, bf16)
        ),
        in_specs=[hbm, pl.BlockSpec(memory_space=pltpu.SMEM), hbm, hbm, hbm, hbm],
        out_specs=(vmem, vmem),
        scratch_shapes=[
            pltpu.VMEM((layers, query_width), bf16),
            pltpu.VMEM((1, src_rows), i32),
            pltpu.VMEM((1, src_rows), i32),
            pltpu.VMEM((layers, src_rows, full), bf16),
            pltpu.VMEM((layers, text_dev, full), bf16),
            pltpu.VMEM((layers, groups, per, main_width), bf16),
            pltpu.VMEM((layers, groups, per, main_width), bf16),
            pltpu.VMEM((groups, layers, per, HEAD_DIM), bf16),
            pltpu.VMEM((groups, layers, per, HEAD_DIM), bf16),
            pltpu.VMEM((1, src_rows), i32),
            pltpu.VMEM((groups, 1, src_rows), i32),
            pltpu.VMEM((layers, rows_padded, text_dev), f32),
            pltpu.VMEM((layers, rows_padded, src_rows), f32),
            pltpu.VMEM((rows_padded, kvw + 2 * HEAD_DIM), f32),
            pltpu.VMEM((rows_padded, main_width - kvw), f32),
            pltpu.VMEM((layers, seq_count, PAD, 3 * HEAD_DIM), f32),
            pltpu.VMEM((layers, seq_count, PAD, 3 * HEAD_DIM), f32),
            dma((3,)), dma((layers,)), dma((layers,)),
            dma((layers, hops)), dma((layers, hops)), dma((hops,)), dma((hops,)),
            dma((hops,)), dma((hops,)), dma((layers, seq_count)), dma((layers, seq_count)),
        ],
        compiler_params=pltpu.CompilerParams(
            collective_id=0, has_side_effects=True, vmem_limit_bytes=32 * 1024 * 1024
        ),
    )(
        in_hbm(query.reshape(layers, query_width)), text_len,
        in_hbm(patch_map.reshape(1, src_rows)), in_hbm(image_places.reshape(1, src_rows)),
        in_hbm(image_rows), in_hbm(text_cache),
    )
    attended, cache = pl.pallas_call(
        finish,
        out_shape=(att_shape, cache_shape),
        in_specs=[vmem, vmem],
        out_specs=(vmem, hbm),
        scratch_shapes=[dma((layers,))],
    )(in_vmem(attended), in_vmem(cache))
    return attended.reshape(layers, 1, query_width // seq_count), cache


def solution(mesh):
    dims = tuple(mesh.shape[a] for a in ("patch", "seq", "req"))
    return jax.shard_map(
        functools.partial(body, dims),
        mesh=mesh,
        in_specs=(
            P(None, ("patch", "req"), None),
            P(None, ("patch", "req"), "seq", None),
            P(("patch", "req")),
            P(None, ("patch", "seq", "req"), None),
            P(("patch", "seq", "req")),
            P(("patch", "seq", "req")),
        ),
        out_specs=(P(None, ("patch", "req"), "seq"), P(None, ("patch", "req"), "seq", None)),
        check_vma=False,
    )
```

time: 62.7 us -> 56.1 us (0.89)
  local copies, waits for them, and re-layouts: 5.65 us -> 0 us
    unnamed x8 -> x0, local copies, waits for them, and re-layouts: 5.06 us -> none
    pallas_call x1 -> x2, Pallas kernels: 55.2 us -> 54.6 us  [the longest x1 52.6 us: body(): pl.pallas_call(functools.partial(kernel, dims), out_shape=(pltpu.VMEM(att...]
where the time goes in v2:
time: 56.1 us; the launch traced here: 55.9 us
  Pallas kernels  54.6 us (97%)
  between operations  1.28 us (2%)
    pallas_call x1, Pallas kernels, body(): pl.pallas_call(functools.partial(kernel, dims), out_shape=(pltpu.VMEM(att...  52.6 us
    pallas_call x1, Pallas kernels, body(): pl.pallas_call(finish, out_shape=(att_shape, cache_shape), in_specs=[vmem...  1.94 us

profile of v2, /device:TPU:0, one launch (start us, length us, event | category | flops | bytes accessed | tf_op | source)
XLA Modules:
  0.0 55.9 jit_solution(10254797213346923762)
XLA Ops:
  1.3 52.6 %shard_map.77 = (bf16[4,896]{1,0:T(4,128)(2,1)S(1)}, bf16[4,1,256,1024]{3,2,1,0:T(8,128)(2,1)S(1)}) custom-call(bf16[4,3584]{1,0:T(4,128)(2,1)} %bitcast.4, s32[1]{0:T(128)S(6)} %copy.8.len_ref, s32[1,256]{1,0:T(1,128)} %bitcast.5, s32[1,256]{1,0:T(1,128)} %bitcast.6, bf16[4,256,1024]{2,1,0:T(8,128)(2,1)} %rows_hbm.1, bf16[4,1,768,1024]{3,2,1,0:T(8,128)(2,1)} %text_hbm.1), custom_call_target="tpu_custom_call" | custom-call | tf_op jit(solution)/shard_map/pallas_call | solution.py:318
  53.9 1.9 %shard_map.78 = (bf16[4,896]{1,0:T(4,128)(2,1)}, bf16[4,1,256,1024]{3,2,1,0:T(8,128)(2,1)}) custom-call(bf16[4,896]{1,0:T(4,128)(2,1)S(1)} %get-tuple-element.6.att_ref, bf16[4,1,256,1024]{3,2,1,0:T(8,128)(2,1)S(1)} %get-tuple-element.7.cache_ref), custom_call_target="tpu_custom_call" | custom-call | tf_op jit(solution)/shard_map/pallas_call | solution.py:355

commit v3 on v2

--- a/solution.py
+++ b/solution.py
@@ -24,9 +24,9 @@
 
 def kernel(
     dims,
-    query_ref, len_ref, map_hbm, place_hbm, rows_hbm, text_hbm,
+    query_ref, len_hbm, map_hbm, place_hbm, rows_hbm, text_hbm,
     att_ref, cache,
-    query, maps, places, rows, text, main_out, main_in, own_out, own_in, place_out, place_in,
+    query, length, maps, places, rows, text, main_out, main_in, own_out, own_in, place_out, place_in,
     scores, image_ws, text_sums, image_sums, part_out, part_in,
     small_sem, rows_sem, text_sem, main_send, main_recv, own_send, own_recv,
     place_send, place_recv, part_send, part_recv,
@@ -45,33 +45,10 @@
     hops = hop_order(patch_count, req_count)
     f32, bf16 = jnp.float32, jnp.bfloat16
 
-    small = [
-        pltpu.make_async_copy(map_hbm, maps, small_sem.at[0]),
-        pltpu.make_async_copy(place_hbm, places, small_sem.at[1]),
-        pltpu.make_async_copy(query_ref, query, small_sem.at[2]),
-    ]
-    for copy in small:
-        copy.start()
-
-    def rows_copy(l):
-        return pltpu.make_async_copy(rows_hbm.at[l], rows.at[l], rows_sem.at[l])
-
-    def text_copy(l):
-        return pltpu.make_async_copy(text_hbm.at[l, 0], text.at[l], text_sem.at[l])
-
-    for l in range(layers):
-        rows_copy(l).start()
-    for l in range(layers):
-        text_copy(l).start()
-
     def partner(hop):
         p = lax.rem(patch + hop[0], patch_count)
         r = lax.rem(req + hop[1], req_count)
         return p, r
-
-    def lanes_of(d):
-        g = lax.rem(seq + d, seq_count)
-        return pl.ds(pl.multiple_of(kvw + g * HEAD_DIM, HEAD_DIM), HEAD_DIM)
 
     barrier = pltpu.get_barrier_semaphore()
     for hop in hops:
@@ -80,6 +57,27 @@
     for d in range(1, seq_count):
         s = lax.rem(seq + d, seq_count)
         pl.semaphore_signal(barrier, inc=1, device_id=(patch, s, req), device_id_type=MESH)
+
+    small = [
+        pltpu.make_async_copy(map_hbm, maps, small_sem.at[0]),
+        pltpu.make_async_copy(place_hbm, places, small_sem.at[1]),
+        pltpu.make_async_copy(query_ref, query, small_sem.at[2]),
+        pltpu.make_async_copy(len_hbm, length, small_sem.at[3]),
+    ]
+    for copy in small:
+        copy.start()
+
+    def rows_copy(l):
+        return pltpu.make_async_copy(rows_hbm.at[l], rows.at[l], rows_sem.at[l])
+
+    def text_copy(l):
+        return pltpu.make_async_copy(text_hbm.at[l, 0], text.at[l], text_sem.at[l])
+
+    rows_copy(0).start()
+
+    def lanes_of(d):
+        g = lax.rem(seq + d, seq_count)
+        return pl.ds(pl.multiple_of(kvw + g * HEAD_DIM, HEAD_DIM), HEAD_DIM)
 
     owner = lax.broadcasted_iota(jnp.int32, (groups, src_rows), 0)
     row_i = lax.broadcasted_iota(jnp.int32, (src_rows, src_rows), 0)
@@ -127,6 +125,9 @@
 
     for l in range(layers):
         rows_copy(l).wait()
+        if l == 0:
+            for m in range(1, layers):
+                rows_copy(m).start()
         keys = jnp.dot(pick, rows[l, :, :kvw], preferred_element_type=f32).astype(bf16)
         main_out[l, :, :, :kvw] = keys.reshape(groups, per, kvw)
         others = jnp.concatenate(
@@ -155,13 +156,16 @@
     for k, hop in enumerate(hops):
         own_copy(k, hop).start()
     for l in range(layers):
+        text_copy(l).start()
+    for l in range(layers):
         main_in[l, me] = main_out[l, me]
     own_in[me] = own_out[me]
 
     positions = seq * text_dev + lax.broadcasted_iota(
         jnp.int32, (KV_HEADS * PAD, text_dev), 1
     )
-    used = positions < len_ref[0]
+    small[3].wait()
+    used = positions < length[0:1, 0:1]
     zeros = jnp.zeros((PAD, HEAD_DIM), bf16)
     small[2].wait()
     lines = query[...].astype(f32)
@@ -282,15 +286,21 @@
         place_copy(k, hop).wait_send()
 
 
-def finish(att_ref, cache_ref, att_out, cache_out, sem):
-    layers = cache_ref.shape[0]
+def finish(att_ref, cache_ref, att_out, cache_out, sem, small_sem):
+    layers, pieces = sem.shape
+    step = cache_ref.shape[2] // pieces
     copies = [
-        pltpu.make_async_copy(cache_ref.at[l], cache_out.at[l], sem.at[l])
+        pltpu.make_async_copy(
+            cache_ref.at[l, :, i * step:(i + 1) * step],
+            cache_out.at[l, :, i * step:(i + 1) * step],
+            sem.at[l, i],
+        )
         for l in range(layers)
+        for i in range(pieces)
     ]
+    copies.append(pltpu.make_async_copy(att_ref, att_out, small_sem.at[0]))
     for copy in copies:
         copy.start()
-    att_out[...] = att_ref[...]
     for copy in copies:
         copy.wait()
 
@@ -320,10 +330,11 @@
         out_shape=(
             pltpu.VMEM(att_shape.shape, bf16), pltpu.VMEM(cache_shape.shape, bf16)
         ),
-        in_specs=[hbm, pl.BlockSpec(memory_space=pltpu.SMEM), hbm, hbm, hbm, hbm],
+        in_specs=[hbm, pl.BlockSpec(memory_space=pl.ANY), hbm, hbm, hbm, hbm],
         out_specs=(vmem, vmem),
         scratch_shapes=[
             pltpu.VMEM((layers, query_width), bf16),
+            pltpu.VMEM((PAD, HEAD_DIM), i32),
             pltpu.VMEM((1, src_rows), i32),
             pltpu.VMEM((1, src_rows), i32),
             pltpu.VMEM((layers, src_rows, full), bf16),
@@ -340,7 +351,7 @@
             pltpu.VMEM((rows_padded, main_width - kvw), f32),
             pltpu.VMEM((layers, seq_count, PAD, 3 * HEAD_DIM), f32),
             pltpu.VMEM((layers, seq_count, PAD, 3 * HEAD_DIM), f32),
-            dma((3,)), dma((layers,)), dma((layers,)),
+            dma((4,)), dma((layers,)), dma((layers,)),
             dma((layers, hops)), dma((layers, hops)), dma((hops,)), dma((hops,)),
             dma((hops,)), dma((hops,)), dma((layers, seq_count)), dma((layers, seq_count)),
         ],
@@ -348,7 +359,7 @@
             collective_id=0, has_side_effects=True, vmem_limit_bytes=32 * 1024 * 1024
         ),
     )(
-        in_hbm(query.reshape(layers, query_width)), text_len,
+        in_hbm(query.reshape(layers, query_width)), jnp.broadcast_to(text_len.reshape(1, 1), (PAD, HEAD_DIM)),
         in_hbm(patch_map.reshape(1, src_rows)), in_hbm(image_places.reshape(1, src_rows)),
         in_hbm(image_rows), in_hbm(text_cache),
     )
@@ -356,8 +367,8 @@
         finish,
         out_shape=(att_shape, cache_shape),
         in_specs=[vmem, vmem],
-        out_specs=(vmem, hbm),
-        scratch_shapes=[dma((layers,))],
+        out_specs=(hbm, hbm),
+        scratch_shapes=[dma((layers, 4)), dma((1,))],
     )(in_vmem(attended), in_vmem(cache))
     return attended.reshape(layers, 1, query_width // seq_count), cache
 

time: 56.1 us -> 55.5 us (0.989)
  no operation moved by 1% of the time
where the time goes in v3:
time: 55.5 us; the launch traced here: 55.4 us
  Pallas kernels  54.1 us (97%)
  between operations  1.29 us (2%)
    pallas_call x1, Pallas kernels, body(): pl.pallas_call(functools.partial(kernel, dims), out_shape=(pltpu.VMEM(att...  52.6 us
    pallas_call x1, Pallas kernels, body(): pl.pallas_call(finish, out_shape=(att_shape, cache_shape), in_specs=[vmem...  1.45 us

profile of v3, /device:TPU:0, one launch (start us, length us, event | category | flops | bytes accessed | tf_op | source)
XLA Modules:
  0.0 55.4 jit_solution(1955004564856247076)
XLA Ops:
  1.3 52.6 %shard_map.77 = (bf16[4,896]{1,0:T(4,128)(2,1)S(1)}, bf16[4,1,256,1024]{3,2,1,0:T(8,128)(2,1)S(1)}) custom-call(bf16[4,3584]{1,0:T(4,128)(2,1)} %bitcast.6, s32[8,128]{1,0:T(8,128)S(1)} %broadcast_in_dim.8.len_hbm, s32[1,256]{1,0:T(1,128)} %bitcast.7, s32[1,256]{1,0:T(1,128)} %bitcast.8, bf16[4,256,1024]{2,1,0:T(8,128)(2,1)} %rows_hbm.1, ...), custom_call_target="tpu_custom_call" | custom-call | tf_op jit(solution)/shard_map/pallas_call | solution.py:328
  53.9 1.5 %shard_map.78 = (bf16[4,896]{1,0:T(4,128)(2,1)}, bf16[4,1,256,1024]{3,2,1,0:T(8,128)(2,1)}) custom-call(bf16[4,896]{1,0:T(4,128)(2,1)S(1)} %get-tuple-element.6.att_ref, bf16[4,1,256,1024]{3,2,1,0:T(8,128)(2,1)S(1)} %get-tuple-element.7.cache_ref), custom_call_target="tpu_custom_call" | custom-call | tf_op jit(solution)/shard_map/pallas_call | solution.py:366
  (1 shorter events, 0.0 us)
